TPU v7x, 32 devices: a whole 2x2x4 slice. The times are simulated.
32 devices in a mesh: blk: 8 (over z, x), grp: 4 (over y, core).
Axes of the slice: x: 2, y: 2, z: 4, core: 2. Of those that a mesh axis runs over, the one named last changes fastest.
Arguments:
- source_coords: float32 [3, 20480], P(None, ('blk', 'grp')), may hold values from 0 to 8, as said below
- source_values: float32 [3, 20480], P(None, ('blk', 'grp')), may hold values from -48 to 48
- target_coords: float32 [3, 16384], P(None, ('blk', 'grp')), may hold values from 0 to 8, as said below
- target_owner: int32 [16384], P(('blk', 'grp')), may hold values from 0 to 7, as said below
Outputs:
- weights: float32 [3, 20480], P(None, ('blk', 'grp'))
- poly: float32 [3, 4], replicated
- mapped: float32 [3, 16384], P(None, ('blk', 'grp'))
Inputs may be any that keep to these rules, and one draw needn't show every extreme that they name: `source_coords`: source vertex j has its first coordinate between j // 2560 and j // 2560 + 1, and the other two between 0 and 1. `target_coords`: target vertex t has its first coordinate between target_owner[t] and target_owner[t] + 1, and the other two between 0 and 1. target_owner[t] differs from t // 2048 by at most one.
All inputs are finite; a program needn't handle non-finite values.
Results may differ from a plain program's by a relative error of at most 0.0003.
Values sent between devices are 32-bit elements; how exact they have to be, the bound alone decides.
A program may use at most 64 MiB of HBM per device.

v0:
```python
import math
import jax
import jax.numpy as jnp
from jax import lax
from jax.sharding import PartitionSpec as P

ITERS = 3
REACH = 2
precise = lax.Precision.HIGHEST
thin_factor = 0.6
tiny = 1e-06


def from_behind(value, axis, steps):
    count = lax.axis_size(axis)
    initial, last = (max(0, -steps), min(count, count - steps))
    return lax.ppermute(value, axis, [(source, source + steps) for source in range(initial, last)])


def kernel_tile(rows, cols, stretch):
    along = rows[0][None, :] - cols[0][:, None]
    across = rows[1][None, :] - cols[1][:, None]
    upward = rows[2][None, :] - cols[2][:, None]
    return jnp.exp(-(thin_factor * along * along + stretch * (across * across + upward * upward)))


def basis(points, partitions, sources):
    ones = jnp.ones_like(points[0])
    stacked = jnp.stack(
        [ones, 2.0 * points[0] / partitions - 1.0, 2.0 * points[1] - 1.0, 2.0 * points[2] - 1.0]
    )
    return stacked / math.sqrt(sources)


def least_squares(hessenberg, beta):
    count = len(hessenberg)
    right_side = [beta] + [jnp.zeros_like(beta) for k in range(count)]
    upper = []
    cosines = []
    sines = []
    for k in range(count):
        column = list(hessenberg[k])
        for i in range(k):
            top = cosines[i] * column[i] + sines[i] * column[i + 1]
            lower = -sines[i] * column[i] + cosines[i] * column[i + 1]
            column[i] = top
            column[i + 1] = lower
        radius = jnp.sqrt(column[k] * column[k] + column[k + 1] * column[k + 1])
        cosine = column[k] / radius
        sine = column[k + 1] / radius
        column[k] = radius
        cosines.append(cosine)
        sines.append(sine)
        right_side[k + 1] = -sine * right_side[k]
        right_side[k] = cosine * right_side[k]
        upper.append(column[: k + 1])
    solved = [None] * count
    for k in reversed(range(count)):
        running = right_side[k]
        for j in range(k + 1, count):
            running = running - upper[j][k] * solved[j]
        solved[k] = running / upper[k][k]
    return solved


def near_slabs(block, reach):
    slab = lax.all_gather(block, "grp", axis=1, tiled=True)
    pieces = []
    for offset in range(-reach, reach + 1):
        if offset == 0:
            pieces.append(slab)
        else:
            pieces.append(from_behind(slab, "blk", -offset))
    return jnp.stack(pieces)


def apply_near(rows, near_coords, near_values, owners, first_slab, stretch, reach):
    labels = jnp.arange(near_coords.shape[0], dtype=jnp.int32) + first_slab

    def add_slab(running, item):
        cols, values, slab = item
        tile = kernel_tile(rows, cols, stretch)
        if owners is not None:
            tile = jnp.where((jnp.abs(owners - slab) <= reach)[None, :], tile, 0.0)
        return (
            running + jnp.dot(values, tile, precision=precise, preferred_element_type=jnp.float32),
            None,
        )

    start = jnp.zeros((near_values.shape[1], rows.shape[1]), jnp.float32)
    result, unused = lax.scan(add_slab, start, (near_coords, near_values, labels))
    return result


def shards(source_coords, source_values, target_coords, target_owner):
    reach = REACH
    own_rows = source_coords.shape[1]
    slab_len = own_rows * lax.axis_size("grp")
    partitions = lax.axis_size("blk")
    sources = slab_len * partitions
    stretch = 4.0 * slab_len
    here = lax.axis_index("blk")
    poly_src = basis(source_coords, partitions, sources)
    start_sq, start_moment = lax.psum(
        (
            jnp.sum(source_values * source_values, axis=1),
            jnp.dot(
                source_values, poly_src.T, precision=precise, preferred_element_type=jnp.float32
            ),
        ),
        ("blk", "grp"),
    )
    beta = jnp.sqrt(start_sq + tiny)
    heads = [source_values / beta[:, None]]
    tails = [jnp.zeros_like(start_moment)]
    moments = [start_moment / beta[:, None]]
    hessenberg = []
    for k in range(ITERS):
        both_near = near_slabs(jnp.concatenate([source_coords, heads[k]], axis=0), reach)
        cols = both_near[:, :3]
        values_near = both_near[:, 3:]
        image_head = apply_near(
            source_coords, cols, values_near, None, here - reach, stretch, reach
        ) + jnp.dot(tails[k], poly_src, precision=precise, preferred_element_type=jnp.float32)
        image_tail = moments[k]
        column = []
        local_dots = jnp.stack(
            [jnp.sum(heads[i] * image_head, axis=1) for i in range(k + 1)], axis=1
        )
        head_dots, image_sq, image_moment = lax.psum(
            (
                local_dots,
                jnp.sum(image_head * image_head, axis=1),
                jnp.dot(
                    image_head, poly_src.T, precision=precise, preferred_element_type=jnp.float32
                ),
            ),
            ("blk", "grp"),
        )
        full_sq = image_sq + jnp.sum(image_tail * image_tail, axis=1)
        rest_head = image_head
        rest_tail = image_tail
        rest_moment = image_moment
        for i in range(k + 1):
            factor = head_dots[:, i] + jnp.sum(tails[i] * image_tail, axis=1)
            full_sq = full_sq - factor * factor
            rest_head = rest_head - factor[:, None] * heads[i]
            rest_tail = rest_tail - factor[:, None] * tails[i]
            rest_moment = rest_moment - factor[:, None] * moments[i]
            column.append(factor)
        length = jnp.sqrt(full_sq + tiny)
        column.append(length)
        hessenberg.append(column)
        heads.append(rest_head / length[:, None])
        tails.append(rest_tail / length[:, None])
        moments.append(rest_moment / length[:, None])
    solved = least_squares(hessenberg, beta)
    weights = solved[0][:, None] * heads[0]
    poly = solved[0][:, None] * tails[0]
    for k in range(1, ITERS):
        weights = weights + solved[k][:, None] * heads[k]
        poly = poly + solved[k][:, None] * tails[k]
    joined_near = near_slabs(jnp.concatenate([source_coords, weights], axis=0), reach + 1)
    cols_far = joined_near[:, :3]
    weights_near = joined_near[:, 3:]
    poly_tgt = basis(target_coords, partitions, sources)
    mapped = apply_near(
        target_coords, cols_far, weights_near, target_owner, here - reach - 1, stretch, reach
    )
    mapped = mapped + jnp.dot(poly, poly_tgt, precision=precise, preferred_element_type=jnp.float32)
    return (weights, poly, mapped)


def solution(mesh):
    return jax.shard_map(
        shards,
        mesh=mesh,
        in_specs=(
            P(None, ("blk", "grp")),
            P(None, ("blk", "grp")),
            P(None, ("blk", "grp")),
            P(("blk", "grp")),
        ),
        out_specs=(P(None, ("blk", "grp")), P(), P(None, ("blk", "grp"))),
        check_vma=False,
    )
```

profile of v0, /device:TPU:6, one launch (start us, length us, event | category | flops | bytes accessed | tf_op | source)
XLA Modules:
  0.0 393.1 jit_solution(17570499681100357009)
XLA Ops:
  1.5 40.3 %psum.70 = f32[3]{0:T(128)S(1)} all-reduce(f32[3]{0:T(128)S(1)} %multiply_reduce_fusion.9), channel_id=1, replica_groups=mesh['blk'=8,'grp'=4] {'blk','grp'}, use_global_device_ids=true, to_apply=%region_1.0 | all-reduce | flops 3 | bytes 24 | tf_op jit(solution)/shard_map/psum | solution.py:104
  64.5 29.7 %while.44 = (s32[]{:T(128)}, f32[3,640]{1,0:T(4,128)S(1)}, f32[5,3,2560]{2,1,0:T(4,128)S(1)}, f32[3,640]{1,0:T(4,128)S(1)}, f32[5,3,2560]{2,1,0:T(4,128)S(1)}, /*index=5*/s32[]{:T(128)}, s32[]{:T(128)}, s32[]{}, s32[]{}) while((s32[]{:T(128)}, f32[3,640]{1,0:T(4,128)S(1)}, f32[5,3,2560]{2,1,0:T(4,128)S(1)}, ...), condition=%wide.region_3.4_spmd.clone, body=%wide.region_2.0_spmd.clone.sunk | while | flops 77008640 | bytes 184975 | solution.py:91
  64.7 5.8 %fusion.163 = f32[3,640]{1,0:T(4,128)S(1)} fusion(f32[2560]{0:T(1024)S(1)} %get-tuple-element.469, f32[640]{0:T(1024)S(1)} %get-tuple-element.470, f32[2560]{0:T(1024)S(1)} %get-tuple-element.471, f32[640]{0:T(1024)S(1)} %get-tuple-element.472, f32[2560]{0:T(1024)S(1)} %get-tuple-element.473, f32[640]{0:T(1024)S(1)} %get-tuple-element.474, ...), kind=kOutput, calls=%fused_computation.20.clone.1 | convolution fusion | flops 77008640 | bytes 108037 | tf_op jit(solution)/shard_map/while/body/eval_jaxpr/dot_general | solution.py:86
  70.6 5.8 %fusion.163 = f32[3,640]{1,0:T(4,128)S(1)} fusion(f32[2560]{0:T(1024)S(1)} %get-tuple-element.469, f32[640]{0:T(1024)S(1)} %get-tuple-element.470, f32[2560]{0:T(1024)S(1)} %get-tuple-element.471, f32[640]{0:T(1024)S(1)} %get-tuple-element.472, f32[2560]{0:T(1024)S(1)} %get-tuple-element.473, f32[640]{0:T(1024)S(1)} %get-tuple-element.474, ...), kind=kOutput, calls=%fused_computation.20.clone.1 | convolution fusion | flops 77008640 | bytes 108037 | tf_op jit(solution)/shard_map/while/body/eval_jaxpr/dot_general | solution.py:86
  76.6 5.8 %fusion.163 = f32[3,640]{1,0:T(4,128)S(1)} fusion(f32[2560]{0:T(1024)S(1)} %get-tuple-element.469, f32[640]{0:T(1024)S(1)} %get-tuple-element.470, f32[2560]{0:T(1024)S(1)} %get-tuple-element.471, f32[640]{0:T(1024)S(1)} %get-tuple-element.472, f32[2560]{0:T(1024)S(1)} %get-tuple-element.473, f32[640]{0:T(1024)S(1)} %get-tuple-element.474, ...), kind=kOutput, calls=%fused_computation.20.clone.1 | convolution fusion | flops 77008640 | bytes 108037 | tf_op jit(solution)/shard_map/while/body/eval_jaxpr/dot_general | solution.py:86
  82.5 5.8 %fusion.163 = f32[3,640]{1,0:T(4,128)S(1)} fusion(f32[2560]{0:T(1024)S(1)} %get-tuple-element.469, f32[640]{0:T(1024)S(1)} %get-tuple-element.470, f32[2560]{0:T(1024)S(1)} %get-tuple-element.471, f32[640]{0:T(1024)S(1)} %get-tuple-element.472, f32[2560]{0:T(1024)S(1)} %get-tuple-element.473, f32[640]{0:T(1024)S(1)} %get-tuple-element.474, ...), kind=kOutput, calls=%fused_computation.20.clone.1 | convolution fusion | flops 77008640 | bytes 108037 | tf_op jit(solution)/shard_map/while/body/eval_jaxpr/dot_general | solution.py:86
  88.4 5.8 %fusion.163 = f32[3,640]{1,0:T(4,128)S(1)} fusion(f32[2560]{0:T(1024)S(1)} %get-tuple-element.469, f32[640]{0:T(1024)S(1)} %get-tuple-element.470, f32[2560]{0:T(1024)S(1)} %get-tuple-element.471, f32[640]{0:T(1024)S(1)} %get-tuple-element.472, f32[2560]{0:T(1024)S(1)} %get-tuple-element.473, f32[640]{0:T(1024)S(1)} %get-tuple-element.474, ...), kind=kOutput, calls=%fused_computation.20.clone.1 | convolution fusion | flops 77008640 | bytes 108037 | tf_op jit(solution)/shard_map/while/body/eval_jaxpr/dot_general | solution.py:86
  94.6 41.4 %all-reduce.2 = (f32[3]{0:T(128)S(1)}, f32[3,4]{1,0:T(4,128)S(1)}, f32[3,1]{0,1:T(1,128)S(1)}) all-reduce(f32[3]{0:T(128)S(1)} %get-tuple-element.232, f32[3,4]{1,0:T(4,128)S(1)} %convolution_bitcast_fusion, f32[3,1]{0,1:T(1,128)S(1)} %bitcast.208), channel_id=1, replica_groups=mesh['blk'=8,'grp'=4] {'blk','grp'}, use_global_device_ids=true, to_apply=%region_9.10 | all-reduce | flops 18 | bytes 144 | tf_op jit(solution)/shard_map/psum | solution.py:130
  155.8 29.7 %while.45 = (s32[]{:T(128)}, f32[3,640]{1,0:T(4,128)S(1)}, f32[5,3,2560]{2,1,0:T(4,128)S(1)}, f32[3,640]{1,0:T(4,128)S(1)}, f32[5,3,2560]{2,1,0:T(4,128)S(1)}, /*index=5*/s32[]{:T(128)}, s32[]{:T(128)}, s32[]{}, s32[]{}) while((s32[]{:T(128)}, f32[3,640]{1,0:T(4,128)S(1)}, f32[5,3,2560]{2,1,0:T(4,128)S(1)}, ...), condition=%wide.region_12.13_spmd.clone, body=%wide.region_11.12_spmd.clone.sunk | while | flops 77008640 | bytes 184975 | solution.py:91
  156.0 5.8 %fusion.166 = f32[3,640]{1,0:T(4,128)S(1)} fusion(f32[2560]{0:T(1024)S(1)} %get-tuple-element.480, f32[640]{0:T(1024)S(1)} %get-tuple-element.481, f32[2560]{0:T(1024)S(1)} %get-tuple-element.482, f32[640]{0:T(1024)S(1)} %get-tuple-element.483, f32[2560]{0:T(1024)S(1)} %get-tuple-element.484, f32[640]{0:T(1024)S(1)} %get-tuple-element.485, ...), kind=kOutput, calls=%fused_computation.52.clone.1 | convolution fusion | flops 77008640 | bytes 108037 | tf_op jit(solution)/shard_map/while/body/eval_jaxpr/dot_general | solution.py:86
  161.9 5.8 %fusion.166 = f32[3,640]{1,0:T(4,128)S(1)} fusion(f32[2560]{0:T(1024)S(1)} %get-tuple-element.480, f32[640]{0:T(1024)S(1)} %get-tuple-element.481, f32[2560]{0:T(1024)S(1)} %get-tuple-element.482, f32[640]{0:T(1024)S(1)} %get-tuple-element.483, f32[2560]{0:T(1024)S(1)} %get-tuple-element.484, f32[640]{0:T(1024)S(1)} %get-tuple-element.485, ...), kind=kOutput, calls=%fused_computation.52.clone.1 | convolution fusion | flops 77008640 | bytes 108037 | tf_op jit(solution)/shard_map/while/body/eval_jaxpr/dot_general | solution.py:86
  167.8 5.8 %fusion.166 = f32[3,640]{1,0:T(4,128)S(1)} fusion(f32[2560]{0:T(1024)S(1)} %get-tuple-element.480, f32[640]{0:T(1024)S(1)} %get-tuple-element.481, f32[2560]{0:T(1024)S(1)} %get-tuple-element.482, f32[640]{0:T(1024)S(1)} %get-tuple-element.483, f32[2560]{0:T(1024)S(1)} %get-tuple-element.484, f32[640]{0:T(1024)S(1)} %get-tuple-element.485, ...), kind=kOutput, calls=%fused_computation.52.clone.1 | convolution fusion | flops 77008640 | bytes 108037 | tf_op jit(solution)/shard_map/while/body/eval_jaxpr/dot_general | solution.py:86
  173.8 5.8 %fusion.166 = f32[3,640]{1,0:T(4,128)S(1)} fusion(f32[2560]{0:T(1024)S(1)} %get-tuple-element.480, f32[640]{0:T(1024)S(1)} %get-tuple-element.481, f32[2560]{0:T(1024)S(1)} %get-tuple-element.482, f32[640]{0:T(1024)S(1)} %get-tuple-element.483, f32[2560]{0:T(1024)S(1)} %get-tuple-element.484, f32[640]{0:T(1024)S(1)} %get-tuple-element.485, ...), kind=kOutput, calls=%fused_computation.52.clone.1 | convolution fusion | flops 77008640 | bytes 108037 | tf_op jit(solution)/shard_map/while/body/eval_jaxpr/dot_general | solution.py:86
  179.7 5.8 %fusion.166 = f32[3,640]{1,0:T(4,128)S(1)} fusion(f32[2560]{0:T(1024)S(1)} %get-tuple-element.480, f32[640]{0:T(1024)S(1)} %get-tuple-element.481, f32[2560]{0:T(1024)S(1)} %get-tuple-element.482, f32[640]{0:T(1024)S(1)} %get-tuple-element.483, f32[2560]{0:T(1024)S(1)} %get-tuple-element.484, f32[640]{0:T(1024)S(1)} %get-tuple-element.485, ...), kind=kOutput, calls=%fused_computation.52.clone.1 | convolution fusion | flops 77008640 | bytes 108037 | tf_op jit(solution)/shard_map/while/body/eval_jaxpr/dot_general | solution.py:86
  185.9 40.5 %all-reduce.1 = (f32[3]{0:T(128)S(1)}, f32[3,4]{1,0:T(4,128)S(1)}, f32[3,2]{0,1:T(2,128)S(1)}) all-reduce(f32[3]{0:T(128)S(1)} %get-tuple-element.229, f32[3,4]{1,0:T(4,128)S(1)} %fusion.135, f32[3,2]{0,1:T(2,128)S(1)} %pad_maximum_fusion.5), channel_id=1, replica_groups=mesh['blk'=8,'grp'=4] {'blk','grp'}, use_global_device_ids=true, to_apply=%region_20.21 | all-reduce | flops 21 | bytes 168 | tf_op jit(solution)/shard_map/psum | solution.py:130
  246.4 29.7 %while.46 = (s32[]{:T(128)}, f32[3,640]{1,0:T(4,128)S(1)}, f32[5,3,2560]{2,1,0:T(4,128)S(1)}, f32[3,640]{1,0:T(4,128)S(1)}, f32[5,3,2560]{2,1,0:T(4,128)S(1)}, /*index=5*/s32[]{:T(128)}, s32[]{:T(128)}, s32[]{}, s32[]{}) while((s32[]{:T(128)}, f32[3,640]{1,0:T(4,128)S(1)}, f32[5,3,2560]{2,1,0:T(4,128)S(1)}, ...), condition=%wide.region_23.24_spmd.clone, body=%wide.region_22.23_spmd.clone.sunk | while | flops 77008640 | bytes 184975 | solution.py:91
  246.5 5.8 %fusion.169 = f32[3,640]{1,0:T(4,128)S(1)} fusion(f32[2560]{0:T(1024)S(1)} %get-tuple-element.491, f32[640]{0:T(1024)S(1)} %get-tuple-element.492, f32[2560]{0:T(1024)S(1)} %get-tuple-element.493, f32[640]{0:T(1024)S(1)} %get-tuple-element.494, f32[2560]{0:T(1024)S(1)} %get-tuple-element.495, f32[640]{0:T(1024)S(1)} %get-tuple-element.496, ...), kind=kOutput, calls=%fused_computation.84.clone.1 | convolution fusion | flops 77008640 | bytes 108037 | tf_op jit(solution)/shard_map/while/body/eval_jaxpr/dot_general | solution.py:86
  252.5 5.8 %fusion.169 = f32[3,640]{1,0:T(4,128)S(1)} fusion(f32[2560]{0:T(1024)S(1)} %get-tuple-element.491, f32[640]{0:T(1024)S(1)} %get-tuple-element.492, f32[2560]{0:T(1024)S(1)} %get-tuple-element.493, f32[640]{0:T(1024)S(1)} %get-tuple-element.494, f32[2560]{0:T(1024)S(1)} %get-tuple-element.495, f32[640]{0:T(1024)S(1)} %get-tuple-element.496, ...), kind=kOutput, calls=%fused_computation.84.clone.1 | convolution fusion | flops 77008640 | bytes 108037 | tf_op jit(solution)/shard_map/while/body/eval_jaxpr/dot_general | solution.py:86
  258.4 5.8 %fusion.169 = f32[3,640]{1,0:T(4,128)S(1)} fusion(f32[2560]{0:T(1024)S(1)} %get-tuple-element.491, f32[640]{0:T(1024)S(1)} %get-tuple-element.492, f32[2560]{0:T(1024)S(1)} %get-tuple-element.493, f32[640]{0:T(1024)S(1)} %get-tuple-element.494, f32[2560]{0:T(1024)S(1)} %get-tuple-element.495, f32[640]{0:T(1024)S(1)} %get-tuple-element.496, ...), kind=kOutput, calls=%fused_computation.84.clone.1 | convolution fusion | flops 77008640 | bytes 108037 | tf_op jit(solution)/shard_map/while/body/eval_jaxpr/dot_general | solution.py:86
  264.3 5.8 %fusion.169 = f32[3,640]{1,0:T(4,128)S(1)} fusion(f32[2560]{0:T(1024)S(1)} %get-tuple-element.491, f32[640]{0:T(1024)S(1)} %get-tuple-element.492, f32[2560]{0:T(1024)S(1)} %get-tuple-element.493, f32[640]{0:T(1024)S(1)} %get-tuple-element.494, f32[2560]{0:T(1024)S(1)} %get-tuple-element.495, f32[640]{0:T(1024)S(1)} %get-tuple-element.496, ...), kind=kOutput, calls=%fused_computation.84.clone.1 | convolution fusion | flops 77008640 | bytes 108037 | tf_op jit(solution)/shard_map/while/body/eval_jaxpr/dot_general | solution.py:86
  270.3 5.8 %fusion.169 = f32[3,640]{1,0:T(4,128)S(1)} fusion(f32[2560]{0:T(1024)S(1)} %get-tuple-element.491, f32[640]{0:T(1024)S(1)} %get-tuple-element.492, f32[2560]{0:T(1024)S(1)} %get-tuple-element.493, f32[640]{0:T(1024)S(1)} %get-tuple-element.494, f32[2560]{0:T(1024)S(1)} %get-tuple-element.495, f32[640]{0:T(1024)S(1)} %get-tuple-element.496, ...), kind=kOutput, calls=%fused_computation.84.clone.1 | convolution fusion | flops 77008640 | bytes 108037 | tf_op jit(solution)/shard_map/while/body/eval_jaxpr/dot_general | solution.py:86
  276.5 41.9 %all-reduce = (f32[3]{0:T(128)S(1)}, f32[3,4]{1,0:T(4,128)S(1)}, f32[3,3]{0,1:T(4,128)S(1)}) all-reduce(f32[3]{0:T(128)S(1)} %get-tuple-element.225, f32[3,4]{1,0:T(4,128)S(1)} %fusion.134, f32[3,3]{0,1:T(4,128)S(1)} %pad_maximum_fusion.4), channel_id=1, replica_groups=mesh['blk'=8,'grp'=4] {'blk','grp'}, use_global_device_ids=true, to_apply=%region_33.34 | all-reduce | flops 24 | bytes 192 | tf_op jit(solution)/shard_map/psum | solution.py:130
  342.9 5.3 %collective-permute-done.17 = f32[6,2560]{1,0:T(8,128)S(1)} collective-permute-done((f32[6,2560]{1,0:T(8,128)S(1)}, f32[6,2560]{1,0:T(8,128)S(1)}, u32[]{:S(2)}, u32[]{:S(2)}) %collective-permute-start.17) | collective-permute-done | bytes 61472 | tf_op jit(solution)/shard_map/ppermute | solution.py:17
  348.9 43.3 %while.47 = (s32[]{:T(128)}, f32[3,512]{1,0:T(4,128)S(1)}, f32[7,3,2560]{2,1,0:T(4,128)S(1)}, s32[7]{0:T(128)S(1)}, s32[512]{0:T(512)S(1)}, /*index=5*/f32[3,512...) while((s32[]{:T(128)}, f32[3,512]{1,0:T(4,128)S(1)}, ...), condition=%wide.region_36.37_spmd.clone, body=%wide.region_35.36_spmd.clone.sunk | while | flops 62919172 | bytes 175279 | solution.py:91
  (178 shorter events, 135.0 us)
Async XLA Ops:
  48.5 13.5 %collective-permute-start = (f32[6,2560]{1,0:T(8,128)S(1)}, f32[6,2560]{1,0:T(8,128)S(1)}, u32[]{:S(2)}, u32[]{:S(2)}) collective-permute-start(f32[6,2560]{1,0:T(8,128)S(1)} %all_gather.12), channel_id=1, source_target_pairs={{0,8},{4,12},{8,16},{12,20},{16,24},{20,28},{1,9},{5,13},{9,17},{1... | collective-permute-start | bytes 184328 | tf_op jit(solution)/shard_map/ppermute | solution.py:17
  52.0 10.1 %collective-permute-start.1 = (f32[6,2560]{1,0:T(8,128)S(1)}, f32[6,2560]{1,0:T(8,128)S(1)}, u32[]{:S(2)}, u32[]{:S(2)}) collective-permute-start(f32[6,2560]{1,0:T(8,128)S(1)} %all_gather.12), channel_id=1, source_target_pairs={{0,4},{4,8},{8,12},{12,16},{16,20},{20,24},{24,28},{1,5},{5,9},{9,... | collective-permute-start | bytes 184328 | tf_op jit(solution)/shard_map/ppermute | solution.py:17
  56.2 7.4 %collective-permute-start.2 = (f32[6,2560]{1,0:T(8,128)S(1)}, f32[6,2560]{1,0:T(8,128)S(1)}, u32[]{:S(2)}, u32[]{:S(2)}) collective-permute-start(f32[6,2560]{1,0:T(8,128)S(1)} %all_gather.12), channel_id=1, source_target_pairs={{4,0},{8,4},{12,8},{16,12},{20,16},{24,20},{28,24},{5,1},{9,5},{13... | collective-permute-start | bytes 184328 | tf_op jit(solution)/shard_map/ppermute | solution.py:17
  58.1 6.3 %collective-permute-start.3 = (f32[6,2560]{1,0:T(8,128)S(1)}, f32[6,2560]{1,0:T(8,128)S(1)}, u32[]{:S(2)}, u32[]{:S(2)}) collective-permute-start(f32[6,2560]{1,0:T(8,128)S(1)} %all_gather.12), channel_id=1, source_target_pairs={{8,0},{12,4},{16,8},{20,12},{24,16},{28,20},{9,1},{13,5},{17,9},{2... | collective-permute-start | bytes 184328 | tf_op jit(solution)/shard_map/ppermute | solution.py:17
  62.1 2.4 copy-start
  64.5 71.7 %copy-start.1 = (f32[3,640]{1,0:T(4,128)S(1)}, f32[3,640]{1,0:T(4,128)}, u32[]{:S(2)}) copy-start(f32[3,640]{1,0:T(4,128)} %param.13) | copy-start | bytes 23044
  141.6 9.5 %collective-permute-start.4 = (f32[6,2560]{1,0:T(8,128)S(1)}, f32[6,2560]{1,0:T(8,128)S(1)}, u32[]{:S(2)}, u32[]{:S(2)}) collective-permute-start(f32[6,2560]{1,0:T(8,128)S(1)} %all_gather.13), channel_id=1, source_target_pairs={{0,8},{4,12},{8,16},{12,20},{16,24},{20,28},{1,9},{5,13},{9,17},{1... | collective-permute-start | bytes 184328 | tf_op jit(solution)/shard_map/ppermute | solution.py:17
  143.5 7.6 %collective-permute-start.5 = (f32[6,2560]{1,0:T(8,128)S(1)}, f32[6,2560]{1,0:T(8,128)S(1)}, u32[]{:S(2)}, u32[]{:S(2)}) collective-permute-start(f32[6,2560]{1,0:T(8,128)S(1)} %all_gather.13), channel_id=1, source_target_pairs={{0,4},{4,8},{8,12},{12,16},{16,20},{20,24},{24,28},{1,5},{5,9},{9,... | collective-permute-start | bytes 184328 | tf_op jit(solution)/shard_map/ppermute | solution.py:17
  146.4 7.4 %collective-permute-start.6 = (f32[6,2560]{1,0:T(8,128)S(1)}, f32[6,2560]{1,0:T(8,128)S(1)}, u32[]{:S(2)}, u32[]{:S(2)}) collective-permute-start(f32[6,2560]{1,0:T(8,128)S(1)} %all_gather.13), channel_id=1, source_target_pairs={{4,0},{8,4},{12,8},{16,12},{20,16},{24,20},{28,24},{5,1},{9,5},{13... | collective-permute-start | bytes 184328 | tf_op jit(solution)/shard_map/ppermute | solution.py:17
  149.4 6.3 %collective-permute-start.7 = (f32[6,2560]{1,0:T(8,128)S(1)}, f32[6,2560]{1,0:T(8,128)S(1)}, u32[]{:S(2)}, u32[]{:S(2)}) collective-permute-start(f32[6,2560]{1,0:T(8,128)S(1)} %all_gather.13), channel_id=1, source_target_pairs={{8,0},{12,4},{16,8},{20,12},{24,16},{28,20},{9,1},{13,5},{17,9},{2... | collective-permute-start | bytes 184328 | tf_op jit(solution)/shard_map/ppermute | solution.py:17
  232.0 9.8 %collective-permute-start.8 = (f32[6,2560]{1,0:T(8,128)S(1)}, f32[6,2560]{1,0:T(8,128)S(1)}, u32[]{:S(2)}, u32[]{:S(2)}) collective-permute-start(f32[6,2560]{1,0:T(8,128)S(1)} %all_gather.14), channel_id=1, source_target_pairs={{0,8},{4,12},{8,16},{12,20},{16,24},{20,28},{1,9},{5,13},{9,17},{1... | collective-permute-start | bytes 184328 | tf_op jit(solution)/shard_map/ppermute | solution.py:17
  234.1 7.7 %collective-permute-start.9 = (f32[6,2560]{1,0:T(8,128)S(1)}, f32[6,2560]{1,0:T(8,128)S(1)}, u32[]{:S(2)}, u32[]{:S(2)}) collective-permute-start(f32[6,2560]{1,0:T(8,128)S(1)} %all_gather.14), channel_id=1, source_target_pairs={{0,4},{4,8},{8,12},{12,16},{16,20},{20,24},{24,28},{1,5},{5,9},{9,... | collective-permute-start | bytes 184328 | tf_op jit(solution)/shard_map/ppermute | solution.py:17
  237.7 7.4 %collective-permute-start.10 = (f32[6,2560]{1,0:T(8,128)S(1)}, f32[6,2560]{1,0:T(8,128)S(1)}, u32[]{:S(2)}, u32[]{:S(2)}) collective-permute-start(f32[6,2560]{1,0:T(8,128)S(1)} %all_gather.14), channel_id=1, source_target_pairs={{4,0},{8,4},{12,8},{16,12},{20,16},{24,20},{28,24},{5,1},{9,5},{13... | collective-permute-start | bytes 184328 | tf_op jit(solution)/shard_map/ppermute | solution.py:17
  240.0 6.3 %collective-permute-start.11 = (f32[6,2560]{1,0:T(8,128)S(1)}, f32[6,2560]{1,0:T(8,128)S(1)}, u32[]{:S(2)}, u32[]{:S(2)}) collective-permute-start(f32[6,2560]{1,0:T(8,128)S(1)} %all_gather.14), channel_id=1, source_target_pairs={{8,0},{12,4},{16,8},{20,12},{24,16},{28,20},{9,1},{13,5},{17,9},{2... | collective-permute-start | bytes 184328 | tf_op jit(solution)/shard_map/ppermute | solution.py:17
  318.8 29.5 %copy-start.4 = (f32[3,640]{1,0:T(4,128)}, f32[3,640]{1,0:T(4,128)S(1)}, u32[]{:S(2)}) copy-start(f32[3,640]{1,0:T(4,128)S(1)} %multiply_add_fusion) | copy-start | bytes 23044
  324.1 13.4 %collective-permute-start.12 = (f32[6,2560]{1,0:T(8,128)S(1)}, f32[6,2560]{1,0:T(8,128)S(1)}, u32[]{:S(2)}, u32[]{:S(2)}) collective-permute-start(f32[6,2560]{1,0:T(8,128)S(1)} %all_gather.15), channel_id=1, source_target_pairs={{0,12},{4,16},{8,20},{12,24},{16,28},{1,13},{5,17},{9,21},{13,25},... | collective-permute-start | bytes 184328 | tf_op jit(solution)/shard_map/ppermute | solution.py:17
  326.3 12.8 %collective-permute-start.13 = (f32[6,2560]{1,0:T(8,128)S(1)}, f32[6,2560]{1,0:T(8,128)S(1)}, u32[]{:S(2)}, u32[]{:S(2)}) collective-permute-start(f32[6,2560]{1,0:T(8,128)S(1)} %all_gather.15), channel_id=1, source_target_pairs={{0,8},{4,12},{8,16},{12,20},{16,24},{20,28},{1,9},{5,13},{9,17},{1... | collective-permute-start | bytes 184328 | tf_op jit(solution)/shard_map/ppermute | solution.py:17
  330.3 8.9 %collective-permute-start.14 = (f32[6,2560]{1,0:T(8,128)S(1)}, f32[6,2560]{1,0:T(8,128)S(1)}, u32[]{:S(2)}, u32[]{:S(2)}) collective-permute-start(f32[6,2560]{1,0:T(8,128)S(1)} %all_gather.15), channel_id=1, source_target_pairs={{0,4},{4,8},{8,12},{12,16},{16,20},{20,24},{24,28},{1,5},{5,9},{9,... | collective-permute-start | bytes 184328 | tf_op jit(solution)/shard_map/ppermute | solution.py:17
  334.1 7.6 %collective-permute-start.15 = (f32[6,2560]{1,0:T(8,128)S(1)}, f32[6,2560]{1,0:T(8,128)S(1)}, u32[]{:S(2)}, u32[]{:S(2)}) collective-permute-start(f32[6,2560]{1,0:T(8,128)S(1)} %all_gather.15), channel_id=1, source_target_pairs={{4,0},{8,4},{12,8},{16,12},{20,16},{24,20},{28,24},{5,1},{9,5},{13... | collective-permute-start | bytes 184328 | tf_op jit(solution)/shard_map/ppermute | solution.py:17
  336.1 6.8 %collective-permute-start.16 = (f32[6,2560]{1,0:T(8,128)S(1)}, f32[6,2560]{1,0:T(8,128)S(1)}, u32[]{:S(2)}, u32[]{:S(2)}) collective-permute-start(f32[6,2560]{1,0:T(8,128)S(1)} %all_gather.15), channel_id=1, source_target_pairs={{8,0},{12,4},{16,8},{20,12},{24,16},{28,20},{9,1},{13,5},{17,9},{2... | collective-permute-start | bytes 184328 | tf_op jit(solution)/shard_map/ppermute | solution.py:17
  337.5 54.8 %copy-start.5 = (f32[3,4]{1,0:T(4,128)}, f32[3,4]{1,0:T(4,128)S(1)}, u32[]{:S(2)}) copy-start(f32[3,4]{1,0:T(4,128)S(1)} %multiply_add_fusion.7) | copy-start | bytes 148
  337.5 10.7 %collective-permute-start.17 = (f32[6,2560]{1,0:T(8,128)S(1)}, f32[6,2560]{1,0:T(8,128)S(1)}, u32[]{:S(2)}, u32[]{:S(2)}) collective-permute-start(f32[6,2560]{1,0:T(8,128)S(1)} %all_gather.15), channel_id=1, source_target_pairs={{12,0},{16,4},{20,8},{24,12},{28,16},{13,1},{17,5},{21,9},{25,13},... | collective-permute-start | bytes 184328 | tf_op jit(solution)/shard_map/ppermute | solution.py:17
  348.2 0.7 copy-start.2
  348.3 0.7 copy-start.3
where the time goes:
time: 395 us; the launch traced here: 393 us
  blocking collectives  185 us (47%)
  matrix products  124 us (31%)
  starting transfers between devices  44.3 us (11%)
  waiting for transfers between devices  20.4 us (5%)
  other arithmetic  9.73 us (2%)
  local copies, waits for them, and re-layouts  7.71 us (2%)
    psum x3, blocking collectives, shards(): lax.psum((local_dots, jnp.sum(image_head * image_head, axis=1), jnp.dot(i...  124 us
    dot_general x22, matrix products, add_slab(): jnp.dot(values, tile, precision=precise, preferred_element_type=jnp.float32)  121 us
    ppermute x18, starting transfers between devices, from_behind(): lax.ppermute(value, axis, [(source, source + steps) for source in range(i...  44.3 us
    psum x1, blocking collectives, shards(): lax.psum((jnp.sum(source_values * source_values, axis=1), jnp.dot(source_...  40.3 us
    all_gather x4, blocking collectives, near_slabs(): slab = lax.all_gather(block, 'grp', axis=1, tiled=True)  21.1 us
    ppermute x18, waiting for transfers between devices, from_behind(): lax.ppermute(value, axis, [(source, source + steps) for source in range(i...  20.4 us
  transfers between devices with their start and end apart: 18, of which 9 were waited for; matrix products, arithmetic and copies ran while one was open for 1% of the time, Pallas kernels for 0%

commit v1 on v0

--- a/solution.py
+++ b/solution.py
@@ -128,14 +128,20 @@
             [jnp.sum(heads[i] * image_head, axis=1) for i in range(k + 1)], axis=1
         )
         head_dots, image_sq, image_moment = lax.psum(
-            (
-                local_dots,
-                jnp.sum(image_head * image_head, axis=1),
-                jnp.dot(
-                    image_head, poly_src.T, precision=precise, preferred_element_type=jnp.float32
+            lax.psum(
+                (
+                    local_dots,
+                    jnp.sum(image_head * image_head, axis=1),
+                    jnp.dot(
+                        image_head,
+                        poly_src.T,
+                        precision=precise,
+                        preferred_element_type=jnp.float32,
+                    ),
                 ),
+                axis_name="grp",
             ),
-            ("blk", "grp"),
+            axis_name="blk",
         )
         full_sq = image_sq + jnp.sum(image_tail * image_tail, axis=1)
         rest_head = image_head

time: 395 us -> 340 us (0.86)
  blocking collectives: 185 us -> 132 us
    psum x3, blocking collectives: 124 us -> 17.2 us  [shards(): lax.psum((local_dots, jnp.sum(image_head * image_head, axis=1), jnp.dot(i...]
    psum x0 -> x3, blocking collectives: none -> 53.7 us  [shards(): lax.psum(lax.psum((local_dots, jnp.sum(image_head * image_head, axis=1),...]
where the time goes in v1:
time: 340 us; the launch traced here: 339 us
  blocking collectives  132 us (39%)
  matrix products  124 us (36%)
  starting transfers between devices  41.2 us (12%)
  waiting for transfers between devices  22 us (6%)
  other arithmetic  9.76 us (3%)
  local copies, waits for them, and re-layouts  7.71 us (2%)
    dot_general x22, matrix products, add_slab(): jnp.dot(values, tile, precision=precise, preferred_element_type=jnp.float32)  121 us
    psum x3, blocking collectives, shards(): lax.psum(lax.psum((local_dots, jnp.sum(image_head * image_head, axis=1),...  53.7 us
    ppermute x18, starting transfers between devices, from_behind(): lax.ppermute(value, axis, [(source, source + steps) for source in range(i...  41.2 us
    psum x1, blocking collectives, shards(): lax.psum((jnp.sum(source_values * source_values, axis=1), jnp.dot(source_...  40.3 us
    ppermute x18, waiting for transfers between devices, from_behind(): lax.ppermute(value, axis, [(source, source + steps) for source in range(i...  22 us
    all_gather x4, blocking collectives, near_slabs(): slab = lax.all_gather(block, 'grp', axis=1, tiled=True)  21.1 us
    psum x3, blocking collectives, shards(): lax.psum((local_dots, jnp.sum(image_head * image_head, axis=1), jnp.dot(i...  17.2 us
  transfers between devices with their start and end apart: 18, of which 9 were waited for; matrix products, arithmetic and copies ran while one was open for 1% of the time, Pallas kernels for 0%

profile of v1, /device:TPU:6, one launch (start us, length us, event | category | flops | bytes accessed | tf_op | source)
XLA Modules:
  0.0 338.7 jit_solution(5934589819539855259)
XLA Ops:
  3.2 40.3 %all-reduce = (f32[3]{0:T(128)S(1)}, f32[3,4]{1,0:T(4,128)S(1)}) all-reduce(f32[3]{0:T(128)S(1)} %multiply_reduce_fusion.9, f32[3,4]{1,0:T(4,128)S(1)} %convolution_bitcast_fusion), channel_id=1, replica_groups=mesh['blk'=8,'grp'=4] {'blk','grp'}, use_global_device_ids=true, to_apply=%region_1.0 | all-reduce | flops 15 | bytes 120 | tf_op jit(solution)/shard_map/psum | solution.py:104
  66.3 29.7 %while.44 = (s32[]{:T(128)}, f32[3,640]{1,0:T(4,128)S(1)}, f32[5,3,2560]{2,1,0:T(4,128)S(1)}, f32[3,640]{1,0:T(4,128)S(1)}, f32[5,3,2560]{2,1,0:T(4,128)S(1)}, /*index=5*/s32[]{:T(128)}, s32[]{:T(128)}, s32[]{}, s32[]{}) while((s32[]{:T(128)}, f32[3,640]{1,0:T(4,128)S(1)}, f32[5,3,2560]{2,1,0:T(4,128)S(1)}, ...), condition=%wide.region_3.4_spmd.clone, body=%wide.region_2.0_spmd.clone.sunk | while | flops 77008640 | bytes 184975 | solution.py:91
  66.5 5.8 %fusion.163 = f32[3,640]{1,0:T(4,128)S(1)} fusion(f32[2560]{0:T(1024)S(1)} %get-tuple-element.478, f32[640]{0:T(1024)S(1)} %get-tuple-element.479, f32[2560]{0:T(1024)S(1)} %get-tuple-element.480, f32[640]{0:T(1024)S(1)} %get-tuple-element.481, f32[2560]{0:T(1024)S(1)} %get-tuple-element.482, f32[640]{0:T(1024)S(1)} %get-tuple-element.483, ...), kind=kOutput, calls=%fused_computation.20.clone.1 | convolution fusion | flops 77008640 | bytes 108037 | tf_op jit(solution)/shard_map/while/body/eval_jaxpr/dot_general | solution.py:86
  72.4 5.8 %fusion.163 = f32[3,640]{1,0:T(4,128)S(1)} fusion(f32[2560]{0:T(1024)S(1)} %get-tuple-element.478, f32[640]{0:T(1024)S(1)} %get-tuple-element.479, f32[2560]{0:T(1024)S(1)} %get-tuple-element.480, f32[640]{0:T(1024)S(1)} %get-tuple-element.481, f32[2560]{0:T(1024)S(1)} %get-tuple-element.482, f32[640]{0:T(1024)S(1)} %get-tuple-element.483, ...), kind=kOutput, calls=%fused_computation.20.clone.1 | convolution fusion | flops 77008640 | bytes 108037 | tf_op jit(solution)/shard_map/while/body/eval_jaxpr/dot_general | solution.py:86
  78.4 5.8 %fusion.163 = f32[3,640]{1,0:T(4,128)S(1)} fusion(f32[2560]{0:T(1024)S(1)} %get-tuple-element.478, f32[640]{0:T(1024)S(1)} %get-tuple-element.479, f32[2560]{0:T(1024)S(1)} %get-tuple-element.480, f32[640]{0:T(1024)S(1)} %get-tuple-element.481, f32[2560]{0:T(1024)S(1)} %get-tuple-element.482, f32[640]{0:T(1024)S(1)} %get-tuple-element.483, ...), kind=kOutput, calls=%fused_computation.20.clone.1 | convolution fusion | flops 77008640 | bytes 108037 | tf_op jit(solution)/shard_map/while/body/eval_jaxpr/dot_general | solution.py:86
  84.3 5.8 %fusion.163 = f32[3,640]{1,0:T(4,128)S(1)} fusion(f32[2560]{0:T(1024)S(1)} %get-tuple-element.478, f32[640]{0:T(1024)S(1)} %get-tuple-element.479, f32[2560]{0:T(1024)S(1)} %get-tuple-element.480, f32[640]{0:T(1024)S(1)} %get-tuple-element.481, f32[2560]{0:T(1024)S(1)} %get-tuple-element.482, f32[640]{0:T(1024)S(1)} %get-tuple-element.483, ...), kind=kOutput, calls=%fused_computation.20.clone.1 | convolution fusion | flops 77008640 | bytes 108037 | tf_op jit(solution)/shard_map/while/body/eval_jaxpr/dot_general | solution.py:86
  90.2 5.8 %fusion.163 = f32[3,640]{1,0:T(4,128)S(1)} fusion(f32[2560]{0:T(1024)S(1)} %get-tuple-element.478, f32[640]{0:T(1024)S(1)} %get-tuple-element.479, f32[2560]{0:T(1024)S(1)} %get-tuple-element.480, f32[640]{0:T(1024)S(1)} %get-tuple-element.481, f32[2560]{0:T(1024)S(1)} %get-tuple-element.482, f32[640]{0:T(1024)S(1)} %get-tuple-element.483, ...), kind=kOutput, calls=%fused_computation.20.clone.1 | convolution fusion | flops 77008640 | bytes 108037 | tf_op jit(solution)/shard_map/while/body/eval_jaxpr/dot_general | solution.py:86
  102.0 18.7 %all-reduce.3 = (f32[3]{0:T(128)S(1)}, f32[3,1]{0,1:T(1,128)S(1)}) all-reduce(f32[3]{0:T(128)S(1)} %get-tuple-element.302, f32[3,1]{0,1:T(1,128)S(1)} %get-tuple-element.303), channel_id=1, replica_groups=mesh['blk'=8,'grp'=4] {'blk'}, use_global_device_ids=true, to_apply=%region_11.12 | all-reduce | flops 6 | bytes 48 | tf_op jit(solution)/shard_map/psum | solution.py:130
  139.7 29.7 %while.45 = (s32[]{:T(128)}, f32[3,640]{1,0:T(4,128)S(1)}, f32[5,3,2560]{2,1,0:T(4,128)S(1)}, f32[3,640]{1,0:T(4,128)S(1)}, f32[5,3,2560]{2,1,0:T(4,128)S(1)}, /*index=5*/s32[]{:T(128)}, s32[]{:T(128)}, s32[]{}, s32[]{}) while((s32[]{:T(128)}, f32[3,640]{1,0:T(4,128)S(1)}, f32[5,3,2560]{2,1,0:T(4,128)S(1)}, ...), condition=%wide.region_14.15_spmd.clone, body=%wide.region_13.14_spmd.clone.sunk | while | flops 77008640 | bytes 184975 | solution.py:91
  139.8 5.8 %fusion.166 = f32[3,640]{1,0:T(4,128)S(1)} fusion(f32[2560]{0:T(1024)S(1)} %get-tuple-element.489, f32[640]{0:T(1024)S(1)} %get-tuple-element.490, f32[2560]{0:T(1024)S(1)} %get-tuple-element.491, f32[640]{0:T(1024)S(1)} %get-tuple-element.492, f32[2560]{0:T(1024)S(1)} %get-tuple-element.493, f32[640]{0:T(1024)S(1)} %get-tuple-element.494, ...), kind=kOutput, calls=%fused_computation.52.clone.1 | convolution fusion | flops 77008640 | bytes 108037 | tf_op jit(solution)/shard_map/while/body/eval_jaxpr/dot_general | solution.py:86
  145.8 5.8 %fusion.166 = f32[3,640]{1,0:T(4,128)S(1)} fusion(f32[2560]{0:T(1024)S(1)} %get-tuple-element.489, f32[640]{0:T(1024)S(1)} %get-tuple-element.490, f32[2560]{0:T(1024)S(1)} %get-tuple-element.491, f32[640]{0:T(1024)S(1)} %get-tuple-element.492, f32[2560]{0:T(1024)S(1)} %get-tuple-element.493, f32[640]{0:T(1024)S(1)} %get-tuple-element.494, ...), kind=kOutput, calls=%fused_computation.52.clone.1 | convolution fusion | flops 77008640 | bytes 108037 | tf_op jit(solution)/shard_map/while/body/eval_jaxpr/dot_general | solution.py:86
  151.7 5.8 %fusion.166 = f32[3,640]{1,0:T(4,128)S(1)} fusion(f32[2560]{0:T(1024)S(1)} %get-tuple-element.489, f32[640]{0:T(1024)S(1)} %get-tuple-element.490, f32[2560]{0:T(1024)S(1)} %get-tuple-element.491, f32[640]{0:T(1024)S(1)} %get-tuple-element.492, f32[2560]{0:T(1024)S(1)} %get-tuple-element.493, f32[640]{0:T(1024)S(1)} %get-tuple-element.494, ...), kind=kOutput, calls=%fused_computation.52.clone.1 | convolution fusion | flops 77008640 | bytes 108037 | tf_op jit(solution)/shard_map/while/body/eval_jaxpr/dot_general | solution.py:86
  157.6 5.8 %fusion.166 = f32[3,640]{1,0:T(4,128)S(1)} fusion(f32[2560]{0:T(1024)S(1)} %get-tuple-element.489, f32[640]{0:T(1024)S(1)} %get-tuple-element.490, f32[2560]{0:T(1024)S(1)} %get-tuple-element.491, f32[640]{0:T(1024)S(1)} %get-tuple-element.492, f32[2560]{0:T(1024)S(1)} %get-tuple-element.493, f32[640]{0:T(1024)S(1)} %get-tuple-element.494, ...), kind=kOutput, calls=%fused_computation.52.clone.1 | convolution fusion | flops 77008640 | bytes 108037 | tf_op jit(solution)/shard_map/while/body/eval_jaxpr/dot_general | solution.py:86
  163.6 5.8 %fusion.166 = f32[3,640]{1,0:T(4,128)S(1)} fusion(f32[2560]{0:T(1024)S(1)} %get-tuple-element.489, f32[640]{0:T(1024)S(1)} %get-tuple-element.490, f32[2560]{0:T(1024)S(1)} %get-tuple-element.491, f32[640]{0:T(1024)S(1)} %get-tuple-element.492, f32[2560]{0:T(1024)S(1)} %get-tuple-element.493, f32[640]{0:T(1024)S(1)} %get-tuple-element.494, ...), kind=kOutput, calls=%fused_computation.52.clone.1 | convolution fusion | flops 77008640 | bytes 108037 | tf_op jit(solution)/shard_map/while/body/eval_jaxpr/dot_general | solution.py:86
  169.8 5.8 %all-reduce.5 = (f32[3]{0:T(128)S(1)}, f32[3,4]{1,0:T(4,128)S(1)}, f32[3,2]{0,1:T(2,128)S(1)}) all-reduce(f32[3]{0:T(128)S(1)} %get-tuple-element.229, f32[3,4]{1,0:T(4,128)S(1)} %fusion.135, f32[3,2]{0,1:T(2,128)S(1)} %pad_maximum_fusion.5), channel_id=1, replica_groups=mesh['blk'=8,'grp'=4] {'grp'}, use_global_device_ids=true, to_apply=%region_24.25 | all-reduce | flops 21 | bytes 168 | tf_op jit(solution)/shard_map/psum | solution.py:131
  175.5 16.7 %all-reduce.2 = (f32[3]{0:T(128)S(1)}, f32[3,4]{1,0:T(4,128)S(1)}, f32[3,2]{0,1:T(2,128)S(1)}) all-reduce(f32[3]{0:T(128)S(1)} %get-tuple-element.299, f32[3,4]{1,0:T(4,128)S(1)} %get-tuple-element.300, f32[3,2]{0,1:T(2,128)S(1)} %get-tuple-element.301), channel_id=1, replica_groups=mesh['blk'=8,'grp'=4] {'blk'}, use_global_device_ids=true, to_apply=%region_25.26 | all-reduce | flops 21 | bytes 168 | tf_op jit(solution)/shard_map/psum | solution.py:130
  211.5 29.7 %while.46 = (s32[]{:T(128)}, f32[3,640]{1,0:T(4,128)S(1)}, f32[5,3,2560]{2,1,0:T(4,128)S(1)}, f32[3,640]{1,0:T(4,128)S(1)}, f32[5,3,2560]{2,1,0:T(4,128)S(1)}, /*index=5*/s32[]{:T(128)}, s32[]{:T(128)}, s32[]{}, s32[]{}) while((s32[]{:T(128)}, f32[3,640]{1,0:T(4,128)S(1)}, f32[5,3,2560]{2,1,0:T(4,128)S(1)}, ...), condition=%wide.region_28.29_spmd.clone, body=%wide.region_27.28_spmd.clone.sunk | while | flops 77008640 | bytes 184975 | solution.py:91
  211.7 5.8 %fusion.169 = f32[3,640]{1,0:T(4,128)S(1)} fusion(f32[2560]{0:T(1024)S(1)} %get-tuple-element.500, f32[640]{0:T(1024)S(1)} %get-tuple-element.501, f32[2560]{0:T(1024)S(1)} %get-tuple-element.502, f32[640]{0:T(1024)S(1)} %get-tuple-element.503, f32[2560]{0:T(1024)S(1)} %get-tuple-element.504, f32[640]{0:T(1024)S(1)} %get-tuple-element.505, ...), kind=kOutput, calls=%fused_computation.84.clone.1 | convolution fusion | flops 77008640 | bytes 108037 | tf_op jit(solution)/shard_map/while/body/eval_jaxpr/dot_general | solution.py:86
  217.6 5.8 %fusion.169 = f32[3,640]{1,0:T(4,128)S(1)} fusion(f32[2560]{0:T(1024)S(1)} %get-tuple-element.500, f32[640]{0:T(1024)S(1)} %get-tuple-element.501, f32[2560]{0:T(1024)S(1)} %get-tuple-element.502, f32[640]{0:T(1024)S(1)} %get-tuple-element.503, f32[2560]{0:T(1024)S(1)} %get-tuple-element.504, f32[640]{0:T(1024)S(1)} %get-tuple-element.505, ...), kind=kOutput, calls=%fused_computation.84.clone.1 | convolution fusion | flops 77008640 | bytes 108037 | tf_op jit(solution)/shard_map/while/body/eval_jaxpr/dot_general | solution.py:86
  223.5 5.8 %fusion.169 = f32[3,640]{1,0:T(4,128)S(1)} fusion(f32[2560]{0:T(1024)S(1)} %get-tuple-element.500, f32[640]{0:T(1024)S(1)} %get-tuple-element.501, f32[2560]{0:T(1024)S(1)} %get-tuple-element.502, f32[640]{0:T(1024)S(1)} %get-tuple-element.503, f32[2560]{0:T(1024)S(1)} %get-tuple-element.504, f32[640]{0:T(1024)S(1)} %get-tuple-element.505, ...), kind=kOutput, calls=%fused_computation.84.clone.1 | convolution fusion | flops 77008640 | bytes 108037 | tf_op jit(solution)/shard_map/while/body/eval_jaxpr/dot_general | solution.py:86
  229.5 5.8 %fusion.169 = f32[3,640]{1,0:T(4,128)S(1)} fusion(f32[2560]{0:T(1024)S(1)} %get-tuple-element.500, f32[640]{0:T(1024)S(1)} %get-tuple-element.501, f32[2560]{0:T(1024)S(1)} %get-tuple-element.502, f32[640]{0:T(1024)S(1)} %get-tuple-element.503, f32[2560]{0:T(1024)S(1)} %get-tuple-element.504, f32[640]{0:T(1024)S(1)} %get-tuple-element.505, ...), kind=kOutput, calls=%fused_computation.84.clone.1 | convolution fusion | flops 77008640 | bytes 108037 | tf_op jit(solution)/shard_map/while/body/eval_jaxpr/dot_general | solution.py:86
  235.4 5.8 %fusion.169 = f32[3,640]{1,0:T(4,128)S(1)} fusion(f32[2560]{0:T(1024)S(1)} %get-tuple-element.500, f32[640]{0:T(1024)S(1)} %get-tuple-element.501, f32[2560]{0:T(1024)S(1)} %get-tuple-element.502, f32[640]{0:T(1024)S(1)} %get-tuple-element.503, f32[2560]{0:T(1024)S(1)} %get-tuple-element.504, f32[640]{0:T(1024)S(1)} %get-tuple-element.505, ...), kind=kOutput, calls=%fused_computation.84.clone.1 | convolution fusion | flops 77008640 | bytes 108037 | tf_op jit(solution)/shard_map/while/body/eval_jaxpr/dot_general | solution.py:86
  247.4 18.4 %all-reduce.1 = (f32[3]{0:T(128)S(1)}, f32[3,4]{1,0:T(4,128)S(1)}, f32[3,3]{0,1:T(4,128)S(1)}) all-reduce(f32[3]{0:T(128)S(1)} %get-tuple-element.296, f32[3,4]{1,0:T(4,128)S(1)} %get-tuple-element.297, f32[3,3]{0,1:T(4,128)S(1)} %get-tuple-element.298), channel_id=1, replica_groups=mesh['blk'=8,'grp'=4] {'blk'}, use_global_device_ids=true, to_apply=%region_41.42 | all-reduce | flops 24 | bytes 192 | tf_op jit(solution)/shard_map/psum | solution.py:130
  294.6 43.3 %while.47 = (s32[]{:T(128)}, f32[3,512]{1,0:T(4,128)S(1)}, f32[7,3,2560]{2,1,0:T(4,128)S(1)}, s32[7]{0:T(128)S(1)}, s32[512]{0:T(512)S(1)}, /*index=5*/f32[3,512...) while((s32[]{:T(128)}, f32[3,512]{1,0:T(4,128)S(1)}, ...), condition=%wide.region_44.45_spmd.clone, body=%wide.region_43.44_spmd.clone.sunk | while | flops 62919172 | bytes 175279 | solution.py:91
  (181 shorter events, 150.3 us)
Async XLA Ops:
  50.3 11.9 %collective-permute-start = (f32[6,2560]{1,0:T(8,128)S(1)}, f32[6,2560]{1,0:T(8,128)S(1)}, u32[]{:S(2)}, u32[]{:S(2)}) collective-permute-start(f32[6,2560]{1,0:T(8,128)S(1)} %all_gather.12), channel_id=1, source_target_pairs={{0,8},{4,12},{8,16},{12,20},{16,24},{20,28},{1,9},{5,13},{9,17},{1... | collective-permute-start | bytes 184328 | tf_op jit(solution)/shard_map/ppermute | solution.py:17
  53.7 8.5 %collective-permute-start.1 = (f32[6,2560]{1,0:T(8,128)S(1)}, f32[6,2560]{1,0:T(8,128)S(1)}, u32[]{:S(2)}, u32[]{:S(2)}) collective-permute-start(f32[6,2560]{1,0:T(8,128)S(1)} %all_gather.12), channel_id=1, source_target_pairs={{0,4},{4,8},{8,12},{12,16},{16,20},{20,24},{24,28},{1,5},{5,9},{9,... | collective-permute-start | bytes 184328 | tf_op jit(solution)/shard_map/ppermute | solution.py:17
  58.0 7.4 %collective-permute-start.2 = (f32[6,2560]{1,0:T(8,128)S(1)}, f32[6,2560]{1,0:T(8,128)S(1)}, u32[]{:S(2)}, u32[]{:S(2)}) collective-permute-start(f32[6,2560]{1,0:T(8,128)S(1)} %all_gather.12), channel_id=1, source_target_pairs={{4,0},{8,4},{12,8},{16,12},{20,16},{24,20},{28,24},{5,1},{9,5},{13... | collective-permute-start | bytes 184328 | tf_op jit(solution)/shard_map/ppermute | solution.py:17
  59.9 6.3 %collective-permute-start.3 = (f32[6,2560]{1,0:T(8,128)S(1)}, f32[6,2560]{1,0:T(8,128)S(1)}, u32[]{:S(2)}, u32[]{:S(2)}) collective-permute-start(f32[6,2560]{1,0:T(8,128)S(1)} %all_gather.12), channel_id=1, source_target_pairs={{8,0},{12,4},{16,8},{20,12},{24,16},{28,20},{9,1},{13,5},{17,9},{2... | collective-permute-start | bytes 184328 | tf_op jit(solution)/shard_map/ppermute | solution.py:17
  62.3 4.0 %copy-start = (f32[3,640]{1,0:T(4,128)S(1)}, f32[3,640]{1,0:T(4,128)}, u32[]{:S(2)}) copy-start(f32[3,640]{1,0:T(4,128)} %param.12) | copy-start | bytes 23044
  66.3 54.4 %copy-start.1 = (f32[3,640]{1,0:T(4,128)S(1)}, f32[3,640]{1,0:T(4,128)}, u32[]{:S(2)}) copy-start(f32[3,640]{1,0:T(4,128)} %param.13) | copy-start | bytes 23044
  126.1 8.8 %collective-permute-start.4 = (f32[6,2560]{1,0:T(8,128)S(1)}, f32[6,2560]{1,0:T(8,128)S(1)}, u32[]{:S(2)}, u32[]{:S(2)}) collective-permute-start(f32[6,2560]{1,0:T(8,128)S(1)} %all_gather.13), channel_id=1, source_target_pairs={{0,8},{4,12},{8,16},{12,20},{16,24},{20,28},{1,9},{5,13},{9,17},{1... | collective-permute-start | bytes 184328 | tf_op jit(solution)/shard_map/ppermute | solution.py:17
  127.4 7.6 %collective-permute-start.5 = (f32[6,2560]{1,0:T(8,128)S(1)}, f32[6,2560]{1,0:T(8,128)S(1)}, u32[]{:S(2)}, u32[]{:S(2)}) collective-permute-start(f32[6,2560]{1,0:T(8,128)S(1)} %all_gather.13), channel_id=1, source_target_pairs={{0,4},{4,8},{8,12},{12,16},{16,20},{20,24},{24,28},{1,5},{5,9},{9,... | collective-permute-start | bytes 184328 | tf_op jit(solution)/shard_map/ppermute | solution.py:17
  129.3 7.5 %collective-permute-start.6 = (f32[6,2560]{1,0:T(8,128)S(1)}, f32[6,2560]{1,0:T(8,128)S(1)}, u32[]{:S(2)}, u32[]{:S(2)}) collective-permute-start(f32[6,2560]{1,0:T(8,128)S(1)} %all_gather.13), channel_id=1, source_target_pairs={{4,0},{8,4},{12,8},{16,12},{20,16},{24,20},{28,24},{5,1},{9,5},{13... | collective-permute-start | bytes 184328 | tf_op jit(solution)/shard_map/ppermute | solution.py:17
  133.2 6.3 %collective-permute-start.7 = (f32[6,2560]{1,0:T(8,128)S(1)}, f32[6,2560]{1,0:T(8,128)S(1)}, u32[]{:S(2)}, u32[]{:S(2)}) collective-permute-start(f32[6,2560]{1,0:T(8,128)S(1)} %all_gather.13), channel_id=1, source_target_pairs={{8,0},{12,4},{16,8},{20,12},{24,16},{28,20},{9,1},{13,5},{17,9},{2... | collective-permute-start | bytes 184328 | tf_op jit(solution)/shard_map/ppermute | solution.py:17
  197.9 9.0 %collective-permute-start.8 = (f32[6,2560]{1,0:T(8,128)S(1)}, f32[6,2560]{1,0:T(8,128)S(1)}, u32[]{:S(2)}, u32[]{:S(2)}) collective-permute-start(f32[6,2560]{1,0:T(8,128)S(1)} %all_gather.14), channel_id=1, source_target_pairs={{0,8},{4,12},{8,16},{12,20},{16,24},{20,28},{1,9},{5,13},{9,17},{1... | collective-permute-start | bytes 184328 | tf_op jit(solution)/shard_map/ppermute | solution.py:17
  199.2 7.8 %collective-permute-start.9 = (f32[6,2560]{1,0:T(8,128)S(1)}, f32[6,2560]{1,0:T(8,128)S(1)}, u32[]{:S(2)}, u32[]{:S(2)}) collective-permute-start(f32[6,2560]{1,0:T(8,128)S(1)} %all_gather.14), channel_id=1, source_target_pairs={{0,4},{4,8},{8,12},{12,16},{16,20},{20,24},{24,28},{1,5},{5,9},{9,... | collective-permute-start | bytes 184328 | tf_op jit(solution)/shard_map/ppermute | solution.py:17
  202.6 7.2 %collective-permute-start.10 = (f32[6,2560]{1,0:T(8,128)S(1)}, f32[6,2560]{1,0:T(8,128)S(1)}, u32[]{:S(2)}, u32[]{:S(2)}) collective-permute-start(f32[6,2560]{1,0:T(8,128)S(1)} %all_gather.14), channel_id=1, source_target_pairs={{4,0},{8,4},{12,8},{16,12},{20,16},{24,20},{28,24},{5,1},{9,5},{13... | collective-permute-start | bytes 184328 | tf_op jit(solution)/shard_map/ppermute | solution.py:17
  205.1 6.3 %collective-permute-start.11 = (f32[6,2560]{1,0:T(8,128)S(1)}, f32[6,2560]{1,0:T(8,128)S(1)}, u32[]{:S(2)}, u32[]{:S(2)}) collective-permute-start(f32[6,2560]{1,0:T(8,128)S(1)} %all_gather.14), channel_id=1, source_target_pairs={{8,0},{12,4},{16,8},{20,12},{24,16},{28,20},{9,1},{13,5},{17,9},{2... | collective-permute-start | bytes 184328 | tf_op jit(solution)/shard_map/ppermute | solution.py:17
  266.1 27.8 %copy-start.4 = (f32[3,640]{1,0:T(4,128)}, f32[3,640]{1,0:T(4,128)S(1)}, u32[]{:S(2)}) copy-start(f32[3,640]{1,0:T(4,128)S(1)} %multiply_add_fusion) | copy-start | bytes 23044
  271.4 11.6 %collective-permute-start.12 = (f32[6,2560]{1,0:T(8,128)S(1)}, f32[6,2560]{1,0:T(8,128)S(1)}, u32[]{:S(2)}, u32[]{:S(2)}) collective-permute-start(f32[6,2560]{1,0:T(8,128)S(1)} %all_gather.15), channel_id=1, source_target_pairs={{0,12},{4,16},{8,20},{12,24},{16,28},{1,13},{5,17},{9,21},{13,25},... | collective-permute-start | bytes 184328 | tf_op jit(solution)/shard_map/ppermute | solution.py:17
  272.7 11.9 %collective-permute-start.13 = (f32[6,2560]{1,0:T(8,128)S(1)}, f32[6,2560]{1,0:T(8,128)S(1)}, u32[]{:S(2)}, u32[]{:S(2)}) collective-permute-start(f32[6,2560]{1,0:T(8,128)S(1)} %all_gather.15), channel_id=1, source_target_pairs={{0,8},{4,12},{8,16},{12,20},{16,24},{20,28},{1,9},{5,13},{9,17},{1... | collective-permute-start | bytes 184328 | tf_op jit(solution)/shard_map/ppermute | solution.py:17
  275.7 8.9 %collective-permute-start.14 = (f32[6,2560]{1,0:T(8,128)S(1)}, f32[6,2560]{1,0:T(8,128)S(1)}, u32[]{:S(2)}, u32[]{:S(2)}) collective-permute-start(f32[6,2560]{1,0:T(8,128)S(1)} %all_gather.15), channel_id=1, source_target_pairs={{0,4},{4,8},{8,12},{12,16},{16,20},{20,24},{24,28},{1,5},{5,9},{9,... | collective-permute-start | bytes 184328 | tf_op jit(solution)/shard_map/ppermute | solution.py:17
  279.8 7.6 %collective-permute-start.15 = (f32[6,2560]{1,0:T(8,128)S(1)}, f32[6,2560]{1,0:T(8,128)S(1)}, u32[]{:S(2)}, u32[]{:S(2)}) collective-permute-start(f32[6,2560]{1,0:T(8,128)S(1)} %all_gather.15), channel_id=1, source_target_pairs={{4,0},{8,4},{12,8},{16,12},{20,16},{24,20},{28,24},{5,1},{9,5},{13... | collective-permute-start | bytes 184328 | tf_op jit(solution)/shard_map/ppermute | solution.py:17
  281.7 6.7 %collective-permute-start.16 = (f32[6,2560]{1,0:T(8,128)S(1)}, f32[6,2560]{1,0:T(8,128)S(1)}, u32[]{:S(2)}, u32[]{:S(2)}) collective-permute-start(f32[6,2560]{1,0:T(8,128)S(1)} %all_gather.15), channel_id=1, source_target_pairs={{8,0},{12,4},{16,8},{20,12},{24,16},{28,20},{9,1},{13,5},{17,9},{2... | collective-permute-start | bytes 184328 | tf_op jit(solution)/shard_map/ppermute | solution.py:17
  283.1 54.9 %copy-start.5 = (f32[3,4]{1,0:T(4,128)}, f32[3,4]{1,0:T(4,128)S(1)}, u32[]{:S(2)}) copy-start(f32[3,4]{1,0:T(4,128)S(1)} %multiply_add_fusion.7) | copy-start | bytes 148
  283.1 10.8 %collective-permute-start.17 = (f32[6,2560]{1,0:T(8,128)S(1)}, f32[6,2560]{1,0:T(8,128)S(1)}, u32[]{:S(2)}, u32[]{:S(2)}) collective-permute-start(f32[6,2560]{1,0:T(8,128)S(1)} %all_gather.15), channel_id=1, source_target_pairs={{12,0},{16,4},{20,8},{24,12},{28,16},{13,1},{17,5},{21,9},{25,13},... | collective-permute-start | bytes 184328 | tf_op jit(solution)/shard_map/ppermute | solution.py:17
  293.9 0.7 copy-start.2
  293.9 0.7 copy-start.3
